TPU v7x, 32 devices: a whole 2x2x4 slice. The times are simulated.
32 devices in a mesh: grp: 2 (over x), scen: 16 (over z, y, core).
Axes of the slice: x: 2, y: 2, z: 4, core: 2. Of those that a mesh axis runs over, the one named last changes fastest.
Arguments:
- shocks: bfloat16 [32768, 2048], P(('grp', 'scen')), parts along dimension 0, may hold values from -8 to 8
- factor_sens: bfloat16 [2048, 1024], replicated, may hold values from -0.13258252 to 0.13258252
- notional: float32 [1024], replicated, may hold values from -0.25 to 0.25
- moneyness: float32 [1024], replicated, may hold values from -2 to 2
- desk_entity: int32 [64], replicated, may hold values from 0 to 7
- scenario_counts: int32 [32], P(('grp', 'scen')), parts along dimension 0, may hold values from 256 to 1024, as said below
- candidate_ids: int32 [2048], P('grp'), parts along dimension 0, may hold values from 0 to 16383, as said below
Outputs:
- tail_losses: float32 [512], P('grp'), parts along dimension 0
- cand_entity: float32 [2048, 8], P(('grp', 'scen')), parts along dimension 0
There are 2 independent parts, one for each index of `grp`. A program takes and returns all parts, laid end to end along the dimension named above; an argument that names none is the same for every part. Nothing has to cross between parts.
Inputs may be any that keep to these rules, and one draw needn't show every extreme that they name: `scenario_counts`: every block has at least 256 valid scenarios; some block in every draw is full. `candidate_ids`: each id b * 1024 + j names a valid scenario: j is below scenario_counts[b].
All inputs are finite; a program needn't handle non-finite values.
Results may differ from a plain program's by a relative error of at most 0.0003.
Values sent between devices are 32-bit elements; how exact they have to be, the bound alone decides.
A program may use at most 128 MiB of HBM per device.

v0:
```python
import jax
import jax.numpy as jnp
from jax import lax
from jax.sharding import PartitionSpec as P

K = 64
INSTR = 16
ENT = 8
TOPK = 256


def price(rows, factor_sens, notional, moneyness):
    value = jnp.dot(rows, factor_sens, preferred_element_type=jnp.float32)
    inst = notional * (jax.nn.softplus(value + moneyness) - jax.nn.softplus(moneyness))
    return jnp.sum(inst.reshape(rows.shape[0], K, INSTR), axis=2)


def body(shocks, factor_sens, notional, moneyness, desk_entity, scenario_counts, candidate_ids):
    slots = shocks.shape[0]
    count = scenario_counts[0]
    block_rows = min(256, slots)
    turns = slots // block_rows

    def one_block(step, desk_all):
        start = step * block_rows

        def active(unused):
            rows = lax.dynamic_slice_in_dim(shocks, start, block_rows, 0)
            return price(rows, factor_sens, notional, moneyness)

        def skipped(unused):
            return jnp.zeros((block_rows, K), jnp.float32)

        piece = lax.cond(start < count, active, skipped, 0)
        return lax.dynamic_update_slice_in_dim(desk_all, piece, start, 0)

    desk_pnl = lax.fori_loop(0, turns, one_block, jnp.zeros((slots, K), jnp.float32))
    loss = -jnp.sum(desk_pnl, axis=1)
    valid = jnp.arange(slots, dtype=jnp.int32) < count
    local_top = lax.top_k(jnp.where(valid, loss, jnp.float32(-1e30)), TOPK)[0]
    every_list = lax.all_gather(local_top, "scen", axis=0, tiled=True)
    tail_losses = lax.top_k(every_list, TOPK)[0]
    local_ids = candidate_ids - lax.axis_index("scen") * slots
    owned = (local_ids >= 0) & (local_ids < slots)
    clipped = jnp.clip(local_ids, 0, slots - 1)
    onehot = (desk_entity[:, None] == jnp.arange(ENT, dtype=jnp.int32)[None, :]).astype(jnp.float32)
    cand_pnl = lax.psum_scatter(
        jnp.where(owned[:, None], jnp.take(desk_pnl, clipped, axis=0), jnp.float32(0.0)),
        "scen",
        scatter_dimension=0,
        tiled=True,
    )
    cand_entity = -jnp.dot(cand_pnl, onehot, precision=lax.Precision.HIGHEST)
    return (tail_losses, cand_entity)


def solution(mesh):
    return jax.shard_map(
        body,
        mesh=mesh,
        in_specs=(P(("grp", "scen"), None), P(), P(), P(), P(), P(("grp", "scen")), P("grp")),
        out_specs=(P("grp"), P(("grp", "scen"), None)),
        check_vma=False,
    )
```

profile of v0, /device:TPU:0, one launch (start us, length us, event | category | flops | bytes accessed | tf_op | source)
XLA Modules:
  0.0 104.4 jit_solution(15786896003439924886)
XLA Ops:
  7.2 0.0 reduce-scatter.2.cloned.1.call-start
  7.2 0.7 fusion.5
  7.9 0.7 compare_and_fusion.1
  8.6 25.0 %while.13 = (s32[]{:T(128)}, f32[1024,64]{0,1:T(8,128)S(1)}, s32[]{:T(128)}, f32[1024]{0:T(1024)}, bf16[1024,2048]{1,0:T(8,128)(2,1)}, /*index=5*/bf16[2048,1024...) while((s32[]{:T(128)}, f32[1024,64]{0,1:T(8,128)S(1)}, ...), condition=%wide.region_4.5_spmd, body=%wide.region_0.4_spmd.sunk | while | flops 1076353024 | bytes 9654531 | solution.py:37
  9.3 5.6 %conditional.2 = (f32[256,64]{0,1:T(8,128)S(1)}) conditional(s32[]{:T(128)} %convert_element_type.9, () %tuple.42, (f32[1024]{0:T(1024)}, s32[]{:T(128)}, bf16[1024,2048]{1,0:T(8,128)(2,1)}, bf16[2048,1024]{1,0:T(8,128)(2,1)}, f32[1024]{0:T(1024)}) %tuple.43), branch_computations={%region_1.0_spmd, %region_2.3_spmd} | conditional | flops 1076353024 | bytes 9523246 | solution.py:34
  9.3 0.7 compare_select_fusion.1
  10.0 4.3 %fusion.1 = f32[256,1024]{1,0:T(8,128)S(1)} fusion(bf16[2048,1024]{1,0:T(8,128)(2,1)} %get-tuple-element.137, bf16[1024,2048]{1,0:T(8,128)(2,1)} %get-tuple-element.135, s32[]{:T(128)S(6)} %select_n.27, f32[1024]{0:T(1024)S(1)} %compare_select_fusion.1, f32[1024]{0:T(1024)} %get-tuple-element.138, f32[1024]{0:T(1024)} %get-tuple-element.134), kind=kOutput, calls=%fused_computation.4 | convolution fusion | flops 1076101120 | bytes 6303748 | tf_op jit(solution)/shard_map/while/body/eval_jaxpr/cond/branch_1_fun/dot_general | solution.py:13
  14.3 0.3 copy.10
  14.7 0.2 bitcast_reduce_fusion
  15.5 5.6 %conditional.2 = (f32[256,64]{0,1:T(8,128)S(1)}) conditional(s32[]{:T(128)} %convert_element_type.9, () %tuple.42, (f32[1024]{0:T(1024)}, s32[]{:T(128)}, bf16[1024,2048]{1,0:T(8,128)(2,1)}, bf16[2048,1024]{1,0:T(8,128)(2,1)}, f32[1024]{0:T(1024)}) %tuple.43), branch_computations={%region_1.0_spmd, %region_2.3_spmd} | conditional | flops 1076353024 | bytes 9523246 | solution.py:34
  15.6 0.7 compare_select_fusion.1
  16.3 4.3 %fusion.1 = f32[256,1024]{1,0:T(8,128)S(1)} fusion(bf16[2048,1024]{1,0:T(8,128)(2,1)} %get-tuple-element.137, bf16[1024,2048]{1,0:T(8,128)(2,1)} %get-tuple-element.135, s32[]{:T(128)S(6)} %select_n.27, f32[1024]{0:T(1024)S(1)} %compare_select_fusion.1, f32[1024]{0:T(1024)} %get-tuple-element.138, f32[1024]{0:T(1024)} %get-tuple-element.134), kind=kOutput, calls=%fused_computation.4 | convolution fusion | flops 1076101120 | bytes 6303748 | tf_op jit(solution)/shard_map/while/body/eval_jaxpr/cond/branch_1_fun/dot_general | solution.py:13
  20.6 0.3 copy.10
  20.9 0.2 bitcast_reduce_fusion
  21.8 5.6 %conditional.2 = (f32[256,64]{0,1:T(8,128)S(1)}) conditional(s32[]{:T(128)} %convert_element_type.9, () %tuple.42, (f32[1024]{0:T(1024)}, s32[]{:T(128)}, bf16[1024,2048]{1,0:T(8,128)(2,1)}, bf16[2048,1024]{1,0:T(8,128)(2,1)}, f32[1024]{0:T(1024)}) %tuple.43), branch_computations={%region_1.0_spmd, %region_2.3_spmd} | conditional | flops 1076353024 | bytes 9523246 | solution.py:34
  21.8 0.7 compare_select_fusion.1
  22.5 4.3 %fusion.1 = f32[256,1024]{1,0:T(8,128)S(1)} fusion(bf16[2048,1024]{1,0:T(8,128)(2,1)} %get-tuple-element.137, bf16[1024,2048]{1,0:T(8,128)(2,1)} %get-tuple-element.135, s32[]{:T(128)S(6)} %select_n.27, f32[1024]{0:T(1024)S(1)} %compare_select_fusion.1, f32[1024]{0:T(1024)} %get-tuple-element.138, f32[1024]{0:T(1024)} %get-tuple-element.134), kind=kOutput, calls=%fused_computation.4 | convolution fusion | flops 1076101120 | bytes 6303748 | tf_op jit(solution)/shard_map/while/body/eval_jaxpr/cond/branch_1_fun/dot_general | solution.py:13
  26.8 0.3 copy.10
  27.2 0.2 bitcast_reduce_fusion
  28.1 5.6 %conditional.2 = (f32[256,64]{0,1:T(8,128)S(1)}) conditional(s32[]{:T(128)} %convert_element_type.9, () %tuple.42, (f32[1024]{0:T(1024)}, s32[]{:T(128)}, bf16[1024,2048]{1,0:T(8,128)(2,1)}, bf16[2048,1024]{1,0:T(8,128)(2,1)}, f32[1024]{0:T(1024)}) %tuple.43), branch_computations={%region_1.0_spmd, %region_2.3_spmd} | conditional | flops 1076353024 | bytes 9523246 | solution.py:34
  28.1 0.7 compare_select_fusion.1
  28.8 4.3 %fusion.1 = f32[256,1024]{1,0:T(8,128)S(1)} fusion(bf16[2048,1024]{1,0:T(8,128)(2,1)} %get-tuple-element.137, bf16[1024,2048]{1,0:T(8,128)(2,1)} %get-tuple-element.135, s32[]{:T(128)S(6)} %select_n.27, f32[1024]{0:T(1024)S(1)} %compare_select_fusion.1, f32[1024]{0:T(1024)} %get-tuple-element.138, f32[1024]{0:T(1024)} %get-tuple-element.134), kind=kOutput, calls=%fused_computation.4 | convolution fusion | flops 1076101120 | bytes 6303748 | tf_op jit(solution)/shard_map/while/body/eval_jaxpr/cond/branch_1_fun/dot_general | solution.py:13
  33.1 0.3 copy.10
  33.4 0.2 bitcast_reduce_fusion
  33.7 0.0 copy-start
  33.7 0.2 copy.12
  33.9 2.8 %gather_fusion = f32[1024,64]{1,0:T(8,128)S(1)} fusion(f32[1024,64]{1,0:T(8,128)S(1)} %copy.12, s32[1024]{0:T(1024)S(1)} %fusion.5), kind=kCustom, calls=%fused_computation | custom fusion | bytes 528384 | tf_op jit(solution)/shard_map/jit(_take)/gather | solution.py:48
  36.7 1.1 %select_select_fusion = f32[1024,64]{1,0:T(8,128)} fusion(f32[1024,64]{1,0:T(8,128)S(1)} %gather_fusion, pred[1024]{0:T(1024)(128)(4,1)S(1)} %get-tuple-element.177, pred[1024]{0:T(1024)(128)(4,1)S(1)} %get-tuple-element.176), kind=kLoop, calls=%fused_computation.11 | loop fusion | flops 131072 | bytes 526336 | tf_op jit(solution)/shard_map/jit(_where)/select_n | solution.py:48
  37.8 0.0 reduce-scatter.2.cloned.1.call-update
  38.5 4.4 %top_k.14 = (f32[1024]{0:T(1024)S(1)}, s32[1024]{0:T(1024)}) sort(f32[1024]{0:T(1024)S(1)} %negate_select_fusion, s32[1024]{0:T(1024)S(1)} %iota.14), dimensions={0}, to_apply=%region_6.7 | sort | flops 10240 | bytes 16384 | tf_op jit(solution)/shard_map/top_k | solution.py:40
  43.0 20.1 %all-gather = f32[16,1,256]{2,1,0:T(1,128)S(1)} all-gather(f32[1,1,256]{2,1,0:T(1,128)S(1)} %bitcast.9), channel_id=1, replica_groups=mesh['grp'=2,'scen'=16] {'scen'}, dimensions={0}, use_global_device_ids=true | all-gather | bytes 17408 | tf_op jit(solution)/shard_map/all_gather | solution.py:41
  63.1 5.9 %top_k.20 = (f32[4096]{0:T(1024)S(1)}, s32[4096]{0:T(1024)}) sort(f32[4096]{0:T(1024)S(1)} %bitcast.8, s32[4096]{0:T(1024)S(1)} %iota.15), dimensions={0}, to_apply=%region_7.8 | sort | flops 49152 | bytes 65536 | tf_op jit(solution)/shard_map/top_k | solution.py:42
  69.0 0.6 top_k.21
  69.5 26.5 %reduce-scatter.2.cloned.1.call-done = f32[64,64]{1,0:T(8,128)} async-done(((f32[1024,64]{1,0:T(8,128)}), f32[64,64]{1,0:T(8,128)}) %reduce-scatter.2.cloned.1.call-update) | async-done | bytes 16400 | tf_op jit(solution)/shard_map/reduce_scatter | solution.py:47
  96.0 0.0 copy-done
  96.0 1.6 %convolution_negate_fusion = f32[64,8]{0,1:T(8,128)} fusion(f32[64,64]{1,0:T(8,128)} %reduce-scatter.2.cloned.1.call-done, s32[64]{0:T(128)S(1)} %copy-done), kind=kOutput, calls=%fused_computation.10 | convolution fusion | flops 394240 | bytes 18688 | tf_op jit(solution)/shard_map/dot_general | solution.py:53
  (10 shorter events, 0.1 us)
Async XLA Ops:
  7.2 88.8 %reduce-scatter.2.cloned.1.call-start = ((), (), s32[]{:S(2)}) async-start(), calls=%async_computation.1 | async-start | bytes 557056 | tf_op jit(solution)/shard_map/reduce_scatter | solution.py:47
  33.7 62.3 %copy-start = (s32[64]{0:T(128)S(1)}, s32[64]{0:T(128)}, u32[]{:S(2)}) copy-start(s32[64]{0:T(128)} %param.15) | copy-start | bytes 772
Sparse Core Ops, SparseCore 0:
  38.0 57.9 reduce-scatter.1
where the time goes:
time: 105 us; the launch traced here: 104 us
  waiting for transfers between devices  26.5 us (25%)
  blocking collectives  20.1 us (19%)
  matrix products  18.8 us (18%)
  other arithmetic  16.4 us (16%)
  between operations  14.7 us (14%)
  local copies, waits for them, and re-layouts  4.97 us (5%)
  loops' own time  2.9 us (3%)
    reduce_scatter x1, waiting for transfers between devices, body(): lax.psum_scatter(jnp.where(owned[:, None], jnp.take(desk_pnl, clipped, ax...  26.5 us
    all_gather x1, blocking collectives, body(): every_list = lax.all_gather(local_top, 'scen', axis=0, tiled=True)  20.1 us
    dot_general x4, matrix products, price(): value = jnp.dot(rows, factor_sens, preferred_element_type=jnp.float32)  17.2 us
    top_k x1, other arithmetic, body(): tail_losses = lax.top_k(every_list, TOPK)[0]  5.87 us
    top_k x1, other arithmetic, body(): local_top = lax.top_k(jnp.where(valid, loss, jnp.float32(-1e+30)), TOPK)[0]  4.43 us
    gather x1, local copies, waits for them, and re-layouts, body(): jnp.take(desk_pnl, clipped, axis=0)  2.8 us
    select_n x4, other arithmetic, price(): jax.nn.softplus(moneyness)  2.8 us
    another operation x1, loops' own time, body(): lax.fori_loop(0, turns, one_block, jnp.zeros((slots, K), jnp.float32))  2.73 us
  transfers between devices with their start and end apart: 1, of which 1 were waited for; matrix products, arithmetic and copies ran while one was open for 10% of the time, Pallas kernels for 0%

commit v1 on v0

--- a/solution.py
+++ b/solution.py
@@ -7,6 +7,24 @@
 INSTR = 16
 ENT = 8
 TOPK = 256
+
+
+def joined_along(pieces, dim):
+    dims = list(pieces.shape[1:])
+    dims[dim] *= pieces.shape[0]
+    return jnp.moveaxis(pieces, 0, dim).reshape(dims)
+
+
+def collected_by_bits(array, axis):
+    count = lax.axis_size(axis)
+    blocks = array[None]
+    for level in range(count.bit_length() - 1):
+        apart = 1 << level
+        other = lax.ppermute(blocks, axis, [(i, i ^ apart) for i in range(count)])
+        both = jnp.stack([blocks, other])
+        upper = lax.axis_index(axis) >> level & 1
+        blocks = jnp.where(upper == 0, both, both[::-1]).reshape(-1, *array.shape)
+    return blocks
 
 
 def price(rows, factor_sens, notional, moneyness):
@@ -38,7 +56,7 @@
     loss = -jnp.sum(desk_pnl, axis=1)
     valid = jnp.arange(slots, dtype=jnp.int32) < count
     local_top = lax.top_k(jnp.where(valid, loss, jnp.float32(-1e30)), TOPK)[0]
-    every_list = lax.all_gather(local_top, "scen", axis=0, tiled=True)
+    every_list = joined_along(collected_by_bits(local_top, "scen"), 0)
     tail_losses = lax.top_k(every_list, TOPK)[0]
     local_ids = candidate_ids - lax.axis_index("scen") * slots
     owned = (local_ids >= 0) & (local_ids < slots)

time: 105 us -> 112 us (1.067)
  waiting for transfers between devices: 26.5 us -> 48.6 us
  blocking collectives: 20.1 us -> 0 us
  starting transfers between devices: 0.04 us -> 6.3 us
  other arithmetic: 16.4 us -> 15.1 us
    all_gather x1 -> x0, blocking collectives: 20.1 us -> none  [body(): every_list = lax.all_gather(local_top, 'scen', axis=0, tiled=True)]
    reduce_scatter x1, waiting for transfers between devices: 26.5 us -> 43.6 us  [body(): lax.psum_scatter(jnp.where(owned[:, None], jnp.take(desk_pnl, clipped, ax...]
    ppermute x0 -> x4, starting transfers between devices: none -> 6.26 us  [collected_by_bits(): other = lax.ppermute(blocks, axis, [(i, i ^ apart) for i in range(count)])]
    ppermute x0 -> x4, waiting for transfers between devices: none -> 5.06 us  [collected_by_bits(): other = lax.ppermute(blocks, axis, [(i, i ^ apart) for i in range(count)])]
  transfers between devices with their start and end apart: 1 -> 5, of which waited for: 1 -> 4; matrix products, arithmetic and copies ran while one was open for 10% -> 10% of each run, Pallas kernels for 0% -> 0%
where the time goes in v1:
time: 112 us
  waiting for transfers between devices  48.6 us (43%)
  matrix products  18.8 us (17%)
  other arithmetic  15.1 us (13%)
  between operations  14.8 us (13%)
  starting transfers between devices  6.3 us (6%)
  local copies, waits for them, and re-layouts  5.09 us (5%)
  loops' own time  2.9 us (3%)
    reduce_scatter x1, waiting for transfers between devices, body(): lax.psum_scatter(jnp.where(owned[:, None], jnp.take(desk_pnl, clipped, ax...  43.6 us
    dot_general x4, matrix products, price(): value = jnp.dot(rows, factor_sens, preferred_element_type=jnp.float32)  17.2 us
    ppermute x4, starting transfers between devices, collected_by_bits(): other = lax.ppermute(blocks, axis, [(i, i ^ apart) for i in range(count)])  6.26 us
    top_k x1, other arithmetic, body(): tail_losses = lax.top_k(every_list, TOPK)[0]  5.87 us
    ppermute x4, waiting for transfers between devices, collected_by_bits(): other = lax.ppermute(blocks, axis, [(i, i ^ apart) for i in range(count)])  5.06 us
    top_k x1, other arithmetic, body(): local_top = lax.top_k(jnp.where(valid, loss, jnp.float32(-1e+30)), TOPK)[0]  4.43 us
    gather x1, local copies, waits for them, and re-layouts, body(): jnp.take(desk_pnl, clipped, axis=0)  2.81 us
    select_n x4, other arithmetic, price(): jax.nn.softplus(moneyness)  2.8 us
  transfers between devices with their start and end apart: 5, of which 4 were waited for; matrix products, arithmetic and copies ran while one was open for 10% of the time, Pallas kernels for 0%

profile of v1, /device:TPU:0, one launch (start us, length us, event | category | flops | bytes accessed | tf_op | source)
XLA Modules:
  0.0 111.7 jit_solution(10839767022200876874)
XLA Ops:
  7.2 0.0 reduce-scatter.2.cloned.1.call-start
  7.9 0.0 copy-start
  7.9 25.0 %while.13 = (s32[]{:T(128)}, f32[1024,64]{0,1:T(8,128)S(1)}, s32[]{:T(128)}, f32[1024]{0:T(1024)}, bf16[1024,2048]{1,0:T(8,128)(2,1)}, /*index=5*/bf16[2048,1024...) while((s32[]{:T(128)}, f32[1024,64]{0,1:T(8,128)S(1)}, ...), condition=%wide.region_4.5_spmd, body=%wide.region_0.4_spmd.sunk | while | flops 1076353024 | bytes 9654531 | solution.py:55
  8.6 5.6 %conditional.2 = (f32[256,64]{0,1:T(8,128)S(1)}) conditional(s32[]{:T(128)} %convert_element_type.9, () %tuple.43, (f32[1024]{0:T(1024)}, s32[]{:T(128)}, bf16[1024,2048]{1,0:T(8,128)(2,1)}, bf16[2048,1024]{1,0:T(8,128)(2,1)}, f32[1024]{0:T(1024)}) %tuple.44), branch_computations={%region_1.0_spmd, %region_2.3_spmd} | conditional | flops 1076353024 | bytes 9523246 | solution.py:52
  8.6 0.7 compare_select_fusion.1
  9.3 4.3 %fusion.1 = f32[256,1024]{1,0:T(8,128)S(1)} fusion(bf16[2048,1024]{1,0:T(8,128)(2,1)} %get-tuple-element.137, bf16[1024,2048]{1,0:T(8,128)(2,1)} %get-tuple-element.135, s32[]{:T(128)S(6)} %select_n.51, f32[1024]{0:T(1024)S(1)} %compare_select_fusion.1, f32[1024]{0:T(1024)} %get-tuple-element.138, f32[1024]{0:T(1024)} %get-tuple-element.134), kind=kOutput, calls=%fused_computation.4 | convolution fusion | flops 1076101120 | bytes 6303748 | tf_op jit(solution)/shard_map/while/body/eval_jaxpr/cond/branch_1_fun/dot_general | solution.py:31
  13.6 0.3 copy.10
  13.9 0.2 bitcast_reduce_fusion
  14.8 5.6 %conditional.2 = (f32[256,64]{0,1:T(8,128)S(1)}) conditional(s32[]{:T(128)} %convert_element_type.9, () %tuple.43, (f32[1024]{0:T(1024)}, s32[]{:T(128)}, bf16[1024,2048]{1,0:T(8,128)(2,1)}, bf16[2048,1024]{1,0:T(8,128)(2,1)}, f32[1024]{0:T(1024)}) %tuple.44), branch_computations={%region_1.0_spmd, %region_2.3_spmd} | conditional | flops 1076353024 | bytes 9523246 | solution.py:52
  14.9 0.7 compare_select_fusion.1
  15.6 4.3 %fusion.1 = f32[256,1024]{1,0:T(8,128)S(1)} fusion(bf16[2048,1024]{1,0:T(8,128)(2,1)} %get-tuple-element.137, bf16[1024,2048]{1,0:T(8,128)(2,1)} %get-tuple-element.135, s32[]{:T(128)S(6)} %select_n.51, f32[1024]{0:T(1024)S(1)} %compare_select_fusion.1, f32[1024]{0:T(1024)} %get-tuple-element.138, f32[1024]{0:T(1024)} %get-tuple-element.134), kind=kOutput, calls=%fused_computation.4 | convolution fusion | flops 1076101120 | bytes 6303748 | tf_op jit(solution)/shard_map/while/body/eval_jaxpr/cond/branch_1_fun/dot_general | solution.py:31
  19.9 0.3 copy.10
  20.2 0.2 bitcast_reduce_fusion
  21.1 5.6 %conditional.2 = (f32[256,64]{0,1:T(8,128)S(1)}) conditional(s32[]{:T(128)} %convert_element_type.9, () %tuple.43, (f32[1024]{0:T(1024)}, s32[]{:T(128)}, bf16[1024,2048]{1,0:T(8,128)(2,1)}, bf16[2048,1024]{1,0:T(8,128)(2,1)}, f32[1024]{0:T(1024)}) %tuple.44), branch_computations={%region_1.0_spmd, %region_2.3_spmd} | conditional | flops 1076353024 | bytes 9523246 | solution.py:52
  21.1 0.7 compare_select_fusion.1
  21.8 4.3 %fusion.1 = f32[256,1024]{1,0:T(8,128)S(1)} fusion(bf16[2048,1024]{1,0:T(8,128)(2,1)} %get-tuple-element.137, bf16[1024,2048]{1,0:T(8,128)(2,1)} %get-tuple-element.135, s32[]{:T(128)S(6)} %select_n.51, f32[1024]{0:T(1024)S(1)} %compare_select_fusion.1, f32[1024]{0:T(1024)} %get-tuple-element.138, f32[1024]{0:T(1024)} %get-tuple-element.134), kind=kOutput, calls=%fused_computation.4 | convolution fusion | flops 1076101120 | bytes 6303748 | tf_op jit(solution)/shard_map/while/body/eval_jaxpr/cond/branch_1_fun/dot_general | solution.py:31
  26.1 0.3 copy.10
  26.5 0.2 bitcast_reduce_fusion
  27.3 5.6 %conditional.2 = (f32[256,64]{0,1:T(8,128)S(1)}) conditional(s32[]{:T(128)} %convert_element_type.9, () %tuple.43, (f32[1024]{0:T(1024)}, s32[]{:T(128)}, bf16[1024,2048]{1,0:T(8,128)(2,1)}, bf16[2048,1024]{1,0:T(8,128)(2,1)}, f32[1024]{0:T(1024)}) %tuple.44), branch_computations={%region_1.0_spmd, %region_2.3_spmd} | conditional | flops 1076353024 | bytes 9523246 | solution.py:52
  27.4 0.7 compare_select_fusion.1
  28.1 4.3 %fusion.1 = f32[256,1024]{1,0:T(8,128)S(1)} fusion(bf16[2048,1024]{1,0:T(8,128)(2,1)} %get-tuple-element.137, bf16[1024,2048]{1,0:T(8,128)(2,1)} %get-tuple-element.135, s32[]{:T(128)S(6)} %select_n.51, f32[1024]{0:T(1024)S(1)} %compare_select_fusion.1, f32[1024]{0:T(1024)} %get-tuple-element.138, f32[1024]{0:T(1024)} %get-tuple-element.134), kind=kOutput, calls=%fused_computation.4 | convolution fusion | flops 1076101120 | bytes 6303748 | tf_op jit(solution)/shard_map/while/body/eval_jaxpr/cond/branch_1_fun/dot_general | solution.py:31
  32.4 0.3 copy.10
  32.7 0.2 bitcast_reduce_fusion
  32.9 0.0 copy-start.1
  33.0 4.4 %top_k.14 = (f32[1024]{0:T(1024)S(1)}, s32[1024]{0:T(1024)}) sort(f32[1024]{0:T(1024)S(1)} %negate_select_fusion, s32[1024]{0:T(1024)S(1)} %iota.14), dimensions={0}, to_apply=%region_6.7 | sort | flops 10240 | bytes 16384 | tf_op jit(solution)/shard_map/top_k | solution.py:58
  37.4 0.5 collective-permute-start
  37.9 0.0 copy-done
  38.0 0.8 collective-permute-done
  38.8 0.1 rev.12
  38.9 2.9 %collective-permute-start.1 = (f32[2,256]{1,0:T(2,128)S(1)}, f32[2,256]{1,0:T(2,128)S(1)}, u32[]{:S(2)}, u32[]{:S(2)}) collective-permute-start(f32[2,256]{1,0:T(2,128)S(1)} %get-tuple-element.179), channel_id=1, source_target_pairs={{0,2},{1,3},{2,0},{3,1},{4,6},{5,7},{6,4},{7,5},{8,10},{9,11},{10,... | collective-permute-start | bytes 6152 | tf_op jit(solution)/shard_map/ppermute | solution.py:23
  41.8 0.2 copy.12
  42.0 2.8 %gather_fusion = f32[1024,64]{1,0:T(8,128)S(1)} fusion(f32[1024,64]{1,0:T(8,128)S(1)} %copy.12, s32[1024]{0:T(1024)S(1)} %fusion.6), kind=kCustom, calls=%fused_computation | custom fusion | bytes 528384 | tf_op jit(solution)/shard_map/jit(_take)/gather | solution.py:66
  44.8 0.0 collective-permute-done.1
  44.8 1.6 %collective-permute-start.2 = (f32[4,256]{1,0:T(4,128)S(1)}, f32[4,256]{1,0:T(4,128)S(1)}, u32[]{:S(2)}, u32[]{:S(2)}) collective-permute-start(f32[4,256]{1,0:T(4,128)S(1)} %reshape.27), channel_id=1, source_target_pairs={{0,4},{1,5},{2,6},{3,7},{4,0},{5,1},{6,2},{7,3},{8,12},{9,13},{10,... | collective-permute-start | bytes 12296 | tf_op jit(solution)/shard_map/ppermute | solution.py:23
  46.5 1.1 %select_select_fusion = f32[1024,64]{1,0:T(8,128)} fusion(f32[1024,64]{1,0:T(8,128)S(1)} %gather_fusion, pred[1024]{0:T(1024)(128)(4,1)S(1)} %get-tuple-element.177, pred[1024]{0:T(1024)(128)(4,1)S(1)} %get-tuple-element.176), kind=kLoop, calls=%fused_computation.11 | loop fusion | flops 131072 | bytes 526336 | tf_op jit(solution)/shard_map/jit(_where)/select_n | solution.py:66
  47.6 0.0 reduce-scatter.2.cloned.1.call-update
  47.7 0.9 collective-permute-done.2
  48.5 1.2 %collective-permute-start.3 = (f32[8,256]{1,0:T(8,128)S(1)}, f32[8,256]{1,0:T(8,128)S(1)}, u32[]{:S(2)}, u32[]{:S(2)}) collective-permute-start(f32[8,256]{1,0:T(8,128)S(1)} %reshape.28), channel_id=1, source_target_pairs={{0,8},{1,9},{2,10},{3,11},{4,12},{5,13},{6,14},{7,15},{8,0},{9,1},... | collective-permute-start | bytes 24584 | tf_op jit(solution)/shard_map/ppermute | solution.py:23
  49.8 3.4 %collective-permute-done.3 = f32[8,256]{1,0:T(8,128)S(1)} collective-permute-done((f32[8,256]{1,0:T(8,128)S(1)}, f32[8,256]{1,0:T(8,128)S(1)}, u32[]{:S(2)}, u32[]{:S(2)}) %collective-permute-start.3) | collective-permute-done | bytes 8224 | tf_op jit(solution)/shard_map/ppermute | solution.py:23
  53.2 5.9 %top_k.20 = (f32[4096]{0:T(1024)S(1)}, s32[4096]{0:T(1024)}) sort(f32[4096]{0:T(1024)S(1)} %bitcast.19, s32[4096]{0:T(1024)S(1)} %iota.15), dimensions={0}, to_apply=%region_7.8 | sort | flops 49152 | bytes 65536 | tf_op jit(solution)/shard_map/top_k | solution.py:60
  59.1 0.6 top_k.21
  59.6 43.6 %reduce-scatter.2.cloned.1.call-done = f32[64,64]{1,0:T(8,128)} async-done(((f32[1024,64]{1,0:T(8,128)}), f32[64,64]{1,0:T(8,128)}) %reduce-scatter.2.cloned.1.call-update) | async-done | bytes 16400 | tf_op jit(solution)/shard_map/reduce_scatter | solution.py:65
  103.2 0.0 copy-done.1
  103.2 1.6 %convolution_negate_fusion = f32[64,8]{0,1:T(8,128)} fusion(f32[64,64]{1,0:T(8,128)} %reduce-scatter.2.cloned.1.call-done, s32[64]{0:T(128)S(1)} %copy-done.1), kind=kOutput, calls=%fused_computation.10 | convolution fusion | flops 394240 | bytes 18688 | tf_op jit(solution)/shard_map/dot_general | solution.py:71
  (25 shorter events, 0.2 us)
Async XLA Ops:
  7.2 96.0 %reduce-scatter.2.cloned.1.call-start = ((), (), s32[]{:S(2)}) async-start(), calls=%async_computation.1 | async-start | bytes 557056 | tf_op jit(solution)/shard_map/reduce_scatter | solution.py:65
  7.9 30.1 %copy-start = (s32[1024]{0:T(1024)S(1)}, s32[1024]{0:T(1024)}, u32[]{:S(2)}) copy-start(s32[1024]{0:T(1024)} %param.17) | copy-start | bytes 12292
  32.9 70.3 %copy-start.1 = (s32[64]{0:T(128)S(1)}, s32[64]{0:T(128)}, u32[]{:S(2)}) copy-start(s32[64]{0:T(128)} %param.15) | copy-start | bytes 772
  37.4 1.3 %collective-permute-start = (f32[1,256]{1,0:T(1,128)S(1)}, f32[1,256]{1,0:T(1,128)S(1)}, u32[]{:S(2)}, u32[]{:S(2)}) collective-permute-start(f32[1,256]{1,0:T(1,128)S(1)} %bitcast.20), channel_id=1, source_target_pairs={{0,1},{1,0},{2,3},{3,2},{4,5},{5,4},{6,7},{7,6},{8,9},{9,8},{10,11... | collective-permute-start | bytes 3080 | tf_op jit(solution)/shard_map/ppermute | solution.py:23
  38.9 5.9 %collective-permute-start.1 = (f32[2,256]{1,0:T(2,128)S(1)}, f32[2,256]{1,0:T(2,128)S(1)}, u32[]{:S(2)}, u32[]{:S(2)}) collective-permute-start(f32[2,256]{1,0:T(2,128)S(1)} %get-tuple-element.179), channel_id=1, source_target_pairs={{0,2},{1,3},{2,0},{3,1},{4,6},{5,7},{6,4},{7,5},{8,10},{9,11},{10,... | collective-permute-start | bytes 6152 | tf_op jit(solution)/shard_map/ppermute | solution.py:23
  44.8 3.7 %collective-permute-start.2 = (f32[4,256]{1,0:T(4,128)S(1)}, f32[4,256]{1,0:T(4,128)S(1)}, u32[]{:S(2)}, u32[]{:S(2)}) collective-permute-start(f32[4,256]{1,0:T(4,128)S(1)} %reshape.27), channel_id=1, source_target_pairs={{0,4},{1,5},{2,6},{3,7},{4,0},{5,1},{6,2},{7,3},{8,12},{9,13},{10,... | collective-permute-start | bytes 12296 | tf_op jit(solution)/shard_map/ppermute | solution.py:23
  48.5 4.6 %collective-permute-start.3 = (f32[8,256]{1,0:T(8,128)S(1)}, f32[8,256]{1,0:T(8,128)S(1)}, u32[]{:S(2)}, u32[]{:S(2)}) collective-permute-start(f32[8,256]{1,0:T(8,128)S(1)} %reshape.28), channel_id=1, source_target_pairs={{0,8},{1,9},{2,10},{3,11},{4,12},{5,13},{6,14},{7,15},{8,0},{9,1},... | collective-permute-start | bytes 24584 | tf_op jit(solution)/shard_map/ppermute | solution.py:23
Sparse Core Ops, SparseCore 0:
  47.8 55.3 reduce-scatter.1
